TPU v7x, 32 devices: a whole 2x2x4 slice. The times are simulated.
32 devices in a mesh: seq: 8 (over z, y), tp: 4 (over x, core).
Axes of the slice: x: 2, y: 2, z: 4, core: 2. Of those that a mesh axis runs over, the one named last changes fastest.
Arguments:
- queries: bfloat16 [1, 2048, 4096], P(None, 'seq', 'tp'), may hold values from -13 to 13
- key_rows: bfloat16 [1, 2048, 2048], P(None, 'seq', 'tp'), may hold values from -13 to 13
- value_rows: bfloat16 [1, 2048, 2048], P(None, 'seq', 'tp'), may hold values from -6 to 6
- residual: bfloat16 [1, 2048, 3584], P(None, 'seq', 'tp'), may hold values from -6 to 6
- out_weight: bfloat16 [4096, 3584], P('tp')
- post_scale: float32 [3584], P('tp'), may hold values from 0.1 to 1.9
- lengths: int32 [1], replicated, may hold values from 512 to 2047
- owners: int32 [1, 8], replicated, may hold values from 0 to 7, each once within a row
Outputs:
- hidden_out: bfloat16 [1, 2048, 3584], P(None, 'seq', 'tp')
- cache_keys: bfloat16 [1, 4096, 2048], P(None, 'seq', 'tp')
- cache_values: bfloat16 [1, 4096, 2048], P(None, 'seq', 'tp')
Inputs may be any that keep to these rules, and one draw needn't show every extreme that they name: Each row of owners names every number from 0 to 7 once.
All inputs are finite; a program needn't handle non-finite values.
Results may differ from a plain program's by a relative error of at most 0.0083.
Values may be sent and summed in bfloat16 or wider, within the bound.
A program may use at most 64 MiB of HBM per device.

v0:
```python
import jax
import jax.numpy as jnp
from jax import lax
from jax.sharding import PartitionSpec as P

D = 3584
HD = 256
WINDOW = 4096


soft_cap = 50.0
norm_eps = 1e-06


def shifted(x, axis, by):
    peers = lax.axis_size(axis)
    pairs = [(i, i + by) for i in range(peers) if 0 <= i + by < peers]
    return lax.ppermute(x, axis, pairs)


def attend_block(grouped, block_keys, block_values, query_pos, key_pos, state_pair):
    numerator, denominator = state_pair
    seq_count, query_count, kv_local, group_size, head_size = grouped.shape
    keyed_rows = block_keys.reshape(seq_count, block_keys.shape[1], kv_local, head_size)
    valued_rows = block_values.reshape(seq_count, block_values.shape[1], kv_local, head_size)
    scores = jnp.einsum(
        "sqhgd,skhd->shgqk", grouped, keyed_rows, preferred_element_type=jnp.float32
    ) * head_size ** (-0.5)
    capped = soft_cap * jnp.tanh(scores / soft_cap)
    spread = query_pos[:, None] - key_pos[None, :]
    live_mask = (spread >= 0) & (spread < WINDOW) & (key_pos[None, :] >= 0)
    weights = jnp.where(live_mask, jnp.exp(capped), jnp.zeros_like(capped))
    denominator = denominator + jnp.sum(weights, axis=-1)
    numerator = numerator + jnp.einsum(
        "shgqk,skhd->sqhgd",
        weights.astype(jnp.bfloat16),
        valued_rows,
        preferred_element_type=jnp.float32,
    )
    return (numerator, denominator)


def reorder_blocks(blocked, ordering):
    return blocked[ordering]


def local(queries, key_rows, value_rows, residual, out_weight, post_scale, lengths, owners):
    seq_count, shard_len, query_width = queries.shape
    kv_width = key_rows.shape[2]
    kv_local = kv_width // HD
    group_size = query_width // kv_width
    grouped = queries.reshape(seq_count, shard_len, kv_local, group_size, HD)
    position = lax.axis_index("seq")
    seq_devices = lax.axis_size("seq")
    offsets = jnp.arange(shard_len, dtype=jnp.int32)
    query_pos = position * shard_len + offsets
    numerator = jnp.zeros((seq_count, shard_len, kv_local, group_size, HD), jnp.float32)
    denominator = jnp.zeros((seq_count, kv_local, group_size, shard_len), jnp.float32)
    state_pair = attend_block(
        grouped, key_rows, value_rows, query_pos, query_pos, (numerator, denominator)
    )
    hop_count = min(WINDOW // shard_len, seq_devices - 1)
    arrived = []
    current = (key_rows, value_rows)
    for hop_index in range(1, hop_count + 1):
        current = shifted((current[0], current[1]), "seq", 1)
        arrived.append((hop_index, current))
        if len(arrived) == 2 or hop_index == hop_count:
            ordered = arrived[::-1]
            block_keys = jnp.concatenate([member[1][0] for member in ordered], axis=1)
            block_values = jnp.concatenate([member[1][1] for member in ordered], axis=1)
            block_pos = jnp.concatenate(
                [(position - member[0]) * shard_len + offsets for member in ordered]
            )
            state_pair = attend_block(
                grouped, block_keys, block_values, query_pos, block_pos, state_pair
            )
            arrived = []
    numerator, denominator = state_pair
    attended = (numerator / jnp.transpose(denominator, (0, 3, 1, 2))[..., None]).astype(
        jnp.bfloat16
    )
    partial_value = jnp.dot(
        attended.reshape(seq_count * shard_len, query_width),
        out_weight,
        preferred_element_type=jnp.float32,
    )
    partial_value = partial_value.reshape(seq_count, shard_len, out_weight.shape[1])
    branch = lax.psum_scatter(partial_value, "tp", scatter_dimension=2, tiled=True)
    squares = lax.psum(jnp.sum(branch * branch, axis=-1), "tp")
    normed = branch * lax.rsqrt(squares / D + norm_eps)[..., None] * post_scale
    hidden_out = (residual.astype(jnp.float32) + normed).astype(jnp.bfloat16)
    block_rows = shard_len // seq_devices
    slot_span = WINDOW // shard_len
    live_rows = (query_pos[None, :] >= lengths[:, None] - WINDOW) & (
        query_pos[None, :] < lengths[:, None]
    )
    kept_keys = jnp.where(live_rows[..., None], key_rows, jnp.zeros_like(key_rows))
    kept_values = jnp.where(live_rows[..., None], value_rows, jnp.zeros_like(value_rows))
    devices = jnp.arange(seq_devices, dtype=jnp.int32)
    matches = owners[:, :, None] == devices[None, None, :]
    inverse = jnp.sum(
        jnp.where(matches, devices[None, :, None], jnp.zeros_like(devices)[None, :, None]), axis=1
    )
    outgoing_keys = jax.vmap(reorder_blocks)(
        kept_keys.reshape(seq_count, seq_devices, block_rows, kv_width), inverse
    )
    outgoing_values = jax.vmap(reorder_blocks)(
        kept_values.reshape(seq_count, seq_devices, block_rows, kv_width), inverse
    )
    incoming = (
        lax.all_to_all(outgoing_keys, "seq", split_axis=1, concat_axis=1, tiled=True),
        lax.all_to_all(outgoing_values, "seq", split_axis=1, concat_axis=1, tiled=True),
    )
    selector = (
        devices[None, :] % slot_span == jnp.arange(slot_span, dtype=jnp.int32)[:, None]
    ).astype(jnp.bfloat16)
    cache_keys = (
        jnp.einsum("md,sdbf->smbf", selector, incoming[0], preferred_element_type=jnp.float32)
        .astype(jnp.bfloat16)
        .reshape(seq_count, slot_span * block_rows, kv_width)
    )
    cache_values = (
        jnp.einsum("md,sdbf->smbf", selector, incoming[1], preferred_element_type=jnp.float32)
        .astype(jnp.bfloat16)
        .reshape(seq_count, slot_span * block_rows, kv_width)
    )
    return (hidden_out, cache_keys, cache_values)


def solution(mesh):
    placed = (
        P(None, "seq", "tp"),
        P(None, "seq", "tp"),
        P(None, "seq", "tp"),
        P(None, "seq", "tp"),
        P("tp", None),
        P("tp"),
        P(),
        P(),
    )
    return jax.shard_map(
        local,
        mesh=mesh,
        in_specs=placed,
        out_specs=(P(None, "seq", "tp"), P(None, "seq", "tp"), P(None, "seq", "tp")),
        check_vma=False,
    )
```

profile of v0, /device:TPU:0, one launch (start us, length us, event | category | flops | bytes accessed | tf_op | source)
XLA Modules:
  0.0 164.7 jit_solution(413193477934840071)
XLA Ops:
  7.2 4.9 %collective-permute-start = (bf16[1,256,512]{2,1,0:T(8,128)(2,1)}, bf16[1,256,512]{2,1,0:T(8,128)(2,1)S(1)}, u32[]{:S(2)}, u32[]{:S(2)}) collective-permute-start(bf16[1,256,512]{2,1,0:T(8,128)(2,1)} %param.10), channel_id=1, source_target_pairs={{0,4},{4,8},{8,12},{12,16},{16,20},{20,24},{24,28},{1,5},{5,9},{9,... | collective-permute-start | bytes 786440 | tf_op jit(solution)/shard_map/ppermute | solution.py:18
  13.2 3.4 %collective-permute-start.2 = (bf16[1,256,512]{1,2,0:T(8,128)(2,1)S(1)}, bf16[1,256,512]{1,2,0:T(8,128)(2,1)S(1)}, u32[]{:S(2)}, u32[]{:S(2)}) collective-permute-start(bf16[1,256,512]{1,2,0:T(8,128)(2,1)S(1)} %copy.84), channel_id=1, source_target_pairs={{0,4},{4,8},{8,12},{12,16},{16,20},{20,24},{24,28},{1,5},{5,9},{9,... | collective-permute-start | bytes 786440 | tf_op jit(solution)/shard_map/ppermute | solution.py:18
  22.7 3.4 %collective-permute-start.1 = (bf16[1,256,512]{2,1,0:T(8,128)(2,1)S(1)}, bf16[1,256,512]{2,1,0:T(8,128)(2,1)S(1)}, u32[]{:S(2)}, u32[]{:S(2)}) collective-permute-start(bf16[1,256,512]{2,1,0:T(8,128)(2,1)S(1)} %collective-permute-done), channel_id=1, source_target_pairs={{0,4},{4,8},{8,12},{12,16},{16,20},{20,24},{24,28},{1,5},{5,9},{9,... | collective-permute-start | bytes 786440 | tf_op jit(solution)/shard_map/ppermute | solution.py:18
  26.2 4.1 %collective-permute-start.3 = (bf16[1,256,512]{1,2,0:T(8,128)(2,1)S(1)}, bf16[1,256,512]{1,2,0:T(8,128)(2,1)}, u32[]{:S(2)}, u32[]{:S(2)}) collective-permute-start(bf16[1,256,512]{1,2,0:T(8,128)(2,1)S(1)} %collective-permute-done.2), channel_id=1, source_target_pairs={{0,4},{4,8},{8,12},{12,16},{16,20},{20,24},{24,28},{1,5},{5,9},{9,... | collective-permute-start | bytes 786440 | tf_op jit(solution)/shard_map/ppermute | solution.py:18
  33.1 4.4 %collective-permute-start.4 = (bf16[1,256,512]{2,1,0:T(8,128)(2,1)S(1)}, bf16[1,256,512]{2,1,0:T(8,128)(2,1)S(1)}, u32[]{:S(2)}, u32[]{:S(2)}) collective-permute-start(bf16[1,256,512]{2,1,0:T(8,128)(2,1)S(1)} %collective-permute-done.1), channel_id=1, source_target_pairs={{0,4},{4,8},{8,12},{12,16},{16,20},{20,24},{24,28},{1,5},{5,9},{9,... | collective-permute-start | bytes 786440 | tf_op jit(solution)/shard_map/ppermute | solution.py:18
  39.4 5.2 %collective-permute-start.6 = (bf16[1,256,512]{1,2,0:T(8,128)(2,1)}, bf16[1,256,512]{1,2,0:T(8,128)(2,1)}, u32[]{:S(2)}, u32[]{:S(2)}) collective-permute-start(bf16[1,256,512]{1,2,0:T(8,128)(2,1)} %collective-permute-done.3), channel_id=1, source_target_pairs={{0,4},{4,8},{8,12},{12,16},{16,20},{20,24},{24,28},{1,5},{5,9},{9,... | collective-permute-start | bytes 786440 | tf_op jit(solution)/shard_map/ppermute | solution.py:18
  45.6 3.5 %collective-permute-start.5 = (bf16[1,256,512]{2,1,0:T(8,128)(2,1)S(1)}, bf16[1,256,512]{2,1,0:T(8,128)(2,1)S(1)}, u32[]{:S(2)}, u32[]{:S(2)}) collective-permute-start(bf16[1,256,512]{2,1,0:T(8,128)(2,1)S(1)} %collective-permute-done.4), channel_id=1, source_target_pairs={{0,4},{4,8},{8,12},{12,16},{16,20},{20,24},{24,28},{1,5},{5,9},{9,... | collective-permute-start | bytes 786440 | tf_op jit(solution)/shard_map/ppermute | solution.py:18
  50.4 5.1 %collective-permute-start.7 = (bf16[1,256,512]{1,2,0:T(8,128)(2,1)}, bf16[1,256,512]{1,2,0:T(8,128)(2,1)}, u32[]{:S(2)}, u32[]{:S(2)}) collective-permute-start(bf16[1,256,512]{1,2,0:T(8,128)(2,1)} %collective-permute-done.6), channel_id=1, source_target_pairs={{0,4},{4,8},{8,12},{12,16},{16,20},{20,24},{24,28},{1,5},{5,9},{9,... | collective-permute-start | bytes 786440 | tf_op jit(solution)/shard_map/ppermute | solution.py:18
  56.2 4.4 %collective-permute-start.8 = (bf16[1,256,512]{2,1,0:T(8,128)(2,1)S(1)}, bf16[1,256,512]{2,1,0:T(8,128)(2,1)S(1)}, u32[]{:S(2)}, u32[]{:S(2)}) collective-permute-start(bf16[1,256,512]{2,1,0:T(8,128)(2,1)S(1)} %collective-permute-done.5), channel_id=1, source_target_pairs={{0,4},{4,8},{8,12},{12,16},{16,20},{20,24},{24,28},{1,5},{5,9},{9,... | collective-permute-start | bytes 786440 | tf_op jit(solution)/shard_map/ppermute | solution.py:18
  62.8 5.1 %collective-permute-start.10 = (bf16[1,256,512]{1,2,0:T(8,128)(2,1)}, bf16[1,256,512]{1,2,0:T(8,128)(2,1)}, u32[]{:S(2)}, u32[]{:S(2)}) collective-permute-start(bf16[1,256,512]{1,2,0:T(8,128)(2,1)} %collective-permute-done.7), channel_id=1, source_target_pairs={{0,4},{4,8},{8,12},{12,16},{16,20},{20,24},{24,28},{1,5},{5,9},{9,... | collective-permute-start | bytes 786440 | tf_op jit(solution)/shard_map/ppermute | solution.py:18
  68.9 4.0 %collective-permute-start.9 = (bf16[1,256,512]{2,1,0:T(8,128)(2,1)S(1)}, bf16[1,256,512]{2,1,0:T(8,128)(2,1)S(1)}, u32[]{:S(2)}, u32[]{:S(2)}) collective-permute-start(bf16[1,256,512]{2,1,0:T(8,128)(2,1)S(1)} %collective-permute-done.8), channel_id=1, source_target_pairs={{0,4},{4,8},{8,12},{12,16},{16,20},{20,24},{24,28},{1,5},{5,9},{9,... | collective-permute-start | bytes 786440 | tf_op jit(solution)/shard_map/ppermute | solution.py:18
  74.1 4.4 %collective-permute-start.11 = (bf16[1,256,512]{1,2,0:T(8,128)(2,1)}, bf16[1,256,512]{1,2,0:T(8,128)(2,1)S(1)}, u32[]{:S(2)}, u32[]{:S(2)}) collective-permute-start(bf16[1,256,512]{1,2,0:T(8,128)(2,1)} %collective-permute-done.10), channel_id=1, source_target_pairs={{0,4},{4,8},{8,12},{12,16},{16,20},{20,24},{24,28},{1,5},{5,9},{9,... | collective-permute-start | bytes 786440 | tf_op jit(solution)/shard_map/ppermute | solution.py:18
  79.9 2.8 %collective-permute-done.11 = bf16[1,256,512]{1,2,0:T(8,128)(2,1)S(1)} collective-permute-done((bf16[1,256,512]{1,2,0:T(8,128)(2,1)}, bf16[1,256,512]{1,2,0:T(8,128)(2,1)S(1)}, u32[]{:S(2)}, u32[]{:S(2)}) %collective-permute-start.11) | collective-permute-done | bytes 262176 | tf_op jit(solution)/shard_map/ppermute | solution.py:18
  84.7 4.8 %collective-permute-start.13 = (bf16[1,256,512]{2,1,0:T(8,128)(2,1)S(1)}, bf16[1,256,512]{2,1,0:T(8,128)(2,1)S(1)}, u32[]{:S(2)}, u32[]{:S(2)}) collective-permute-start(bf16[1,256,512]{2,1,0:T(8,128)(2,1)S(1)} %copy-done.4), channel_id=1, source_target_pairs={{0,4},{4,8},{8,12},{12,16},{16,20},{20,24},{24,28},{1,5},{5,9},{9,... | collective-permute-start | bytes 786440 | tf_op jit(solution)/shard_map/ppermute | solution.py:18
  89.5 5.2 %collective-permute-start.12 = (bf16[1,256,512]{1,2,0:T(8,128)(2,1)}, bf16[1,256,512]{1,2,0:T(8,128)(2,1)S(1)}, u32[]{:S(2)}, u32[]{:S(2)}) collective-permute-start(bf16[1,256,512]{1,2,0:T(8,128)(2,1)} %copy-done.5), channel_id=1, source_target_pairs={{0,4},{4,8},{8,12},{12,16},{16,20},{20,24},{24,28},{1,5},{5,9},{9,... | collective-permute-start | bytes 786440 | tf_op jit(solution)/shard_map/ppermute | solution.py:18
  95.2 3.7 %collective-permute-done.12 = bf16[1,256,512]{1,2,0:T(8,128)(2,1)S(1)} collective-permute-done((bf16[1,256,512]{1,2,0:T(8,128)(2,1)}, bf16[1,256,512]{1,2,0:T(8,128)(2,1)S(1)}, u32[]{:S(2)}, u32[]{:S(2)}) %collective-permute-start.12) | collective-permute-done | bytes 262176 | tf_op jit(solution)/shard_map/ppermute | solution.py:18
  99.9 7.0 %convolution_bitcast_fusion = f32[1,256,3584]{2,1,0:T(8,128)} fusion(bf16[256,1024]{0,1:T(8,128)(2,1)S(1)} %bitcast.167, bf16[1024,3584]{1,0:T(8,128)(2,1)} %param.12), kind=kOutput, calls=%fused_computation.2 | convolution fusion | flops 1879048192 | bytes 11534336 | tf_op jit(solution)/shard_map/dot_general | solution.py:83
  109.3 5.0 %all-to-all-start = ((bf16[1,8,32,512]{3,2,0,1:T(8,128)(2,1)}), bf16[1,8,32,512]{3,2,0,1:T(8,128)(2,1)S(1)}, u32[]{:S(2)}, u32[]{:S(2)}) async-start(bf16[1,8,32,512]{3,2,0,1:T(8,128)(2,1)} %bitcast.58), calls=%async_computation.1 | async-start | bytes 524288 | tf_op jit(solution)/shard_map/all_to_all | solution.py:112
  115.6 7.0 %all-to-all-done = bf16[1,8,32,512]{3,2,0,1:T(8,128)(2,1)S(1)} async-done(((bf16[1,8,32,512]{3,2,0,1:T(8,128)(2,1)}), bf16[1,8,32,512]{3,2,0,1:T(8,128)(2,1)S(1)}, u32[]{:S(2)}, u32[]{:S(2)}) %all-to-all-start) | async-done | bytes 262176 | tf_op jit(solution)/shard_map/all_to_all | solution.py:112
  122.5 3.4 %all-to-all-start.1 = ((bf16[1,8,32,512]{3,2,0,1:T(8,128)(2,1)}), bf16[1,8,32,512]{3,2,0,1:T(8,128)(2,1)S(1)}, u32[]{:S(2)}, u32[]{:S(2)}) async-start(bf16[1,8,32,512]{3,2,0,1:T(8,128)(2,1)} %bitcast.66), calls=%async_computation.2 | async-start | bytes 524288 | tf_op jit(solution)/shard_map/all_to_all | solution.py:113
  127.5 6.6 %all-to-all-done.1 = bf16[1,8,32,512]{3,2,0,1:T(8,128)(2,1)S(1)} async-done(((bf16[1,8,32,512]{3,2,0,1:T(8,128)(2,1)}), bf16[1,8,32,512]{3,2,0,1:T(8,128)(2,1)S(1)}, u32[]{:S(2)}, u32[]{:S(2)}) %all-to-all-start.1) | async-done | bytes 262176 | tf_op jit(solution)/shard_map/all_to_all | solution.py:113
  135.6 13.0 %reduce-scatter.2.cloned.1.call-done = f32[1,256,896]{2,1,0:T(8,128)} async-done(((f32[1,256,3584]{2,1,0:T(8,128)}), f32[1,256,896]{2,1,0:T(8,128)}) %reduce-scatter.2.cloned.1.call-update) | async-done | bytes 917520 | tf_op jit(solution)/shard_map/reduce_scatter | solution.py:89
  149.9 5.8 %psum.7 = f32[1,256]{1,0:T(1,128)S(1)} all-reduce(f32[1,256]{1,0:T(1,128)S(1)} %bitcast.176), channel_id=1, replica_groups=mesh['seq'=8,'tp'=4] {'tp'}, use_global_device_ids=true, to_apply=%region_7.8 | all-reduce | flops 256 | bytes 2048 | tf_op jit(solution)/shard_map/psum | solution.py:90
  155.7 2.2 %add_convert_fusion = bf16[1,256,896]{2,1,0:T(8,128)(2,1)} fusion(f32[1,256,896]{2,1,0:T(8,128)} %reduce-scatter.2.cloned.1.call-done, bf16[1,256,896]{2,1,0:T(8,128)(2,1)S(1)} %copy-done.2, f32[896]{0:T(1024)S(1)} %copy-done.9, f32[256]{0:T(256)S(1)} %bitcast.175), kind=kLoop, calls=%fused_computation.36 | loop fusion | flops 1146880 | bytes 1839616 | tf_op jit(solution)/shard_map/convert_element_type | solution.py:92
  (89 shorter events, 31.3 us)
Async XLA Ops:
  7.2 141.4 %reduce-scatter.2.cloned.1.call-start = ((), (), s32[]{:S(2)}) async-start(), calls=%async_computation.3 | async-start | bytes 4587520 | tf_op jit(solution)/shard_map/reduce_scatter | solution.py:89
  7.2 15.5 %collective-permute-start = (bf16[1,256,512]{2,1,0:T(8,128)(2,1)}, bf16[1,256,512]{2,1,0:T(8,128)(2,1)S(1)}, u32[]{:S(2)}, u32[]{:S(2)}) collective-permute-start(bf16[1,256,512]{2,1,0:T(8,128)(2,1)} %param.10), channel_id=1, source_target_pairs={{0,4},{4,8},{8,12},{12,16},{16,20},{20,24},{24,28},{1,5},{5,9},{9,... | collective-permute-start | bytes 786440 | tf_op jit(solution)/shard_map/ppermute | solution.py:18
  13.2 12.9 %collective-permute-start.2 = (bf16[1,256,512]{1,2,0:T(8,128)(2,1)S(1)}, bf16[1,256,512]{1,2,0:T(8,128)(2,1)S(1)}, u32[]{:S(2)}, u32[]{:S(2)}) collective-permute-start(bf16[1,256,512]{1,2,0:T(8,128)(2,1)S(1)} %copy.84), channel_id=1, source_target_pairs={{0,4},{4,8},{8,12},{12,16},{16,20},{20,24},{24,28},{1,5},{5,9},{9,... | collective-permute-start | bytes 786440 | tf_op jit(solution)/shard_map/ppermute | solution.py:18
  22.7 10.1 %collective-permute-start.1 = (bf16[1,256,512]{2,1,0:T(8,128)(2,1)S(1)}, bf16[1,256,512]{2,1,0:T(8,128)(2,1)S(1)}, u32[]{:S(2)}, u32[]{:S(2)}) collective-permute-start(bf16[1,256,512]{2,1,0:T(8,128)(2,1)S(1)} %collective-permute-done), channel_id=1, source_target_pairs={{0,4},{4,8},{8,12},{12,16},{16,20},{20,24},{24,28},{1,5},{5,9},{9,... | collective-permute-start | bytes 786440 | tf_op jit(solution)/shard_map/ppermute | solution.py:18
  26.2 12.3 %collective-permute-start.3 = (bf16[1,256,512]{1,2,0:T(8,128)(2,1)S(1)}, bf16[1,256,512]{1,2,0:T(8,128)(2,1)}, u32[]{:S(2)}, u32[]{:S(2)}) collective-permute-start(bf16[1,256,512]{1,2,0:T(8,128)(2,1)S(1)} %collective-permute-done.2), channel_id=1, source_target_pairs={{0,4},{4,8},{8,12},{12,16},{16,20},{20,24},{24,28},{1,5},{5,9},{9,... | collective-permute-start | bytes 786440 | tf_op jit(solution)/shard_map/ppermute | solution.py:18
  32.9 11.8 %copy-start.7 = (pred[256,512]{0,1:T(8,128)(4,1)S(1)}, pred[256,512]{0,1:T(8,128)(4,1)}, u32[]{:S(2)}) copy-start(pred[256,512]{0,1:T(8,128)(4,1)} %get-tuple-element.7) | copy-start | bytes 393220
  33.1 12.5 %collective-permute-start.4 = (bf16[1,256,512]{2,1,0:T(8,128)(2,1)S(1)}, bf16[1,256,512]{2,1,0:T(8,128)(2,1)S(1)}, u32[]{:S(2)}, u32[]{:S(2)}) collective-permute-start(bf16[1,256,512]{2,1,0:T(8,128)(2,1)S(1)} %collective-permute-done.1), channel_id=1, source_target_pairs={{0,4},{4,8},{8,12},{12,16},{16,20},{20,24},{24,28},{1,5},{5,9},{9,... | collective-permute-start | bytes 786440 | tf_op jit(solution)/shard_map/ppermute | solution.py:18
  39.4 10.9 %collective-permute-start.6 = (bf16[1,256,512]{1,2,0:T(8,128)(2,1)}, bf16[1,256,512]{1,2,0:T(8,128)(2,1)}, u32[]{:S(2)}, u32[]{:S(2)}) collective-permute-start(bf16[1,256,512]{1,2,0:T(8,128)(2,1)} %collective-permute-done.3), channel_id=1, source_target_pairs={{0,4},{4,8},{8,12},{12,16},{16,20},{20,24},{24,28},{1,5},{5,9},{9,... | collective-permute-start | bytes 786440 | tf_op jit(solution)/shard_map/ppermute | solution.py:18
  45.6 10.3 %collective-permute-start.5 = (bf16[1,256,512]{2,1,0:T(8,128)(2,1)S(1)}, bf16[1,256,512]{2,1,0:T(8,128)(2,1)S(1)}, u32[]{:S(2)}, u32[]{:S(2)}) collective-permute-start(bf16[1,256,512]{2,1,0:T(8,128)(2,1)S(1)} %collective-permute-done.4), channel_id=1, source_target_pairs={{0,4},{4,8},{8,12},{12,16},{16,20},{20,24},{24,28},{1,5},{5,9},{9,... | collective-permute-start | bytes 786440 | tf_op jit(solution)/shard_map/ppermute | solution.py:18
  50.4 11.4 %collective-permute-start.7 = (bf16[1,256,512]{1,2,0:T(8,128)(2,1)}, bf16[1,256,512]{1,2,0:T(8,128)(2,1)}, u32[]{:S(2)}, u32[]{:S(2)}) collective-permute-start(bf16[1,256,512]{1,2,0:T(8,128)(2,1)} %collective-permute-done.6), channel_id=1, source_target_pairs={{0,4},{4,8},{8,12},{12,16},{16,20},{20,24},{24,28},{1,5},{5,9},{9,... | collective-permute-start | bytes 786440 | tf_op jit(solution)/shard_map/ppermute | solution.py:18
  55.9 12.0 %copy-start.6 = (pred[256,512]{0,1:T(8,128)(4,1)S(1)}, pred[256,512]{0,1:T(8,128)(4,1)}, u32[]{:S(2)}) copy-start(pred[256,512]{0,1:T(8,128)(4,1)} %get-tuple-element.6) | copy-start | bytes 393220
  56.2 12.7 %collective-permute-start.8 = (bf16[1,256,512]{2,1,0:T(8,128)(2,1)S(1)}, bf16[1,256,512]{2,1,0:T(8,128)(2,1)S(1)}, u32[]{:S(2)}, u32[]{:S(2)}) collective-permute-start(bf16[1,256,512]{2,1,0:T(8,128)(2,1)S(1)} %collective-permute-done.5), channel_id=1, source_target_pairs={{0,4},{4,8},{8,12},{12,16},{16,20},{20,24},{24,28},{1,5},{5,9},{9,... | collective-permute-start | bytes 786440 | tf_op jit(solution)/shard_map/ppermute | solution.py:18
  62.8 11.3 %collective-permute-start.10 = (bf16[1,256,512]{1,2,0:T(8,128)(2,1)}, bf16[1,256,512]{1,2,0:T(8,128)(2,1)}, u32[]{:S(2)}, u32[]{:S(2)}) collective-permute-start(bf16[1,256,512]{1,2,0:T(8,128)(2,1)} %collective-permute-done.7), channel_id=1, source_target_pairs={{0,4},{4,8},{8,12},{12,16},{16,20},{20,24},{24,28},{1,5},{5,9},{9,... | collective-permute-start | bytes 786440 | tf_op jit(solution)/shard_map/ppermute | solution.py:18
  68.9 10.1 %collective-permute-start.9 = (bf16[1,256,512]{2,1,0:T(8,128)(2,1)S(1)}, bf16[1,256,512]{2,1,0:T(8,128)(2,1)S(1)}, u32[]{:S(2)}, u32[]{:S(2)}) collective-permute-start(bf16[1,256,512]{2,1,0:T(8,128)(2,1)S(1)} %collective-permute-done.8), channel_id=1, source_target_pairs={{0,4},{4,8},{8,12},{12,16},{16,20},{20,24},{24,28},{1,5},{5,9},{9,... | collective-permute-start | bytes 786440 | tf_op jit(solution)/shard_map/ppermute | solution.py:18
  74.1 8.6 %collective-permute-start.11 = (bf16[1,256,512]{1,2,0:T(8,128)(2,1)}, bf16[1,256,512]{1,2,0:T(8,128)(2,1)S(1)}, u32[]{:S(2)}, u32[]{:S(2)}) collective-permute-start(bf16[1,256,512]{1,2,0:T(8,128)(2,1)} %collective-permute-done.10), channel_id=1, source_target_pairs={{0,4},{4,8},{8,12},{12,16},{16,20},{20,24},{24,28},{1,5},{5,9},{9,... | collective-permute-start | bytes 786440 | tf_op jit(solution)/shard_map/ppermute | solution.py:18
  82.7 1.1 copy-start.5
  84.7 14.2 %copy-start.8 = (pred[256,256]{0,1:T(8,128)(4,1)S(1)}, pred[256,256]{0,1:T(8,128)(4,1)}, u32[]{:S(2)}) copy-start(pred[256,256]{0,1:T(8,128)(4,1)} %get-tuple-element.3) | copy-start | bytes 196612
  84.7 14.7 %collective-permute-start.13 = (bf16[1,256,512]{2,1,0:T(8,128)(2,1)S(1)}, bf16[1,256,512]{2,1,0:T(8,128)(2,1)S(1)}, u32[]{:S(2)}, u32[]{:S(2)}) collective-permute-start(bf16[1,256,512]{2,1,0:T(8,128)(2,1)S(1)} %copy-done.4), channel_id=1, source_target_pairs={{0,4},{4,8},{8,12},{12,16},{16,20},{20,24},{24,28},{1,5},{5,9},{9,... | collective-permute-start | bytes 786440 | tf_op jit(solution)/shard_map/ppermute | solution.py:18
  89.5 9.4 %collective-permute-start.12 = (bf16[1,256,512]{1,2,0:T(8,128)(2,1)}, bf16[1,256,512]{1,2,0:T(8,128)(2,1)S(1)}, u32[]{:S(2)}, u32[]{:S(2)}) collective-permute-start(bf16[1,256,512]{1,2,0:T(8,128)(2,1)} %copy-done.5), channel_id=1, source_target_pairs={{0,4},{4,8},{8,12},{12,16},{16,20},{20,24},{24,28},{1,5},{5,9},{9,... | collective-permute-start | bytes 786440 | tf_op jit(solution)/shard_map/ppermute | solution.py:18
  106.9 1.0 copy-start.1
  109.3 13.2 %all-to-all-start = ((bf16[1,8,32,512]{3,2,0,1:T(8,128)(2,1)}), bf16[1,8,32,512]{3,2,0,1:T(8,128)(2,1)S(1)}, u32[]{:S(2)}, u32[]{:S(2)}) async-start(bf16[1,8,32,512]{3,2,0,1:T(8,128)(2,1)} %bitcast.58), calls=%async_computation.1 | async-start | bytes 524288 | tf_op jit(solution)/shard_map/all_to_all | solution.py:112
  122.5 11.6 %all-to-all-start.1 = ((bf16[1,8,32,512]{3,2,0,1:T(8,128)(2,1)}), bf16[1,8,32,512]{3,2,0,1:T(8,128)(2,1)S(1)}, u32[]{:S(2)}, u32[]{:S(2)}) async-start(bf16[1,8,32,512]{3,2,0,1:T(8,128)(2,1)} %bitcast.66), calls=%async_computation.2 | async-start | bytes 524288 | tf_op jit(solution)/shard_map/all_to_all | solution.py:113
  126.4 29.3 %copy-start.2 = (bf16[1,256,896]{2,1,0:T(8,128)(2,1)S(1)}, bf16[1,256,896]{2,1,0:T(8,128)(2,1)}, u32[]{:S(2)}) copy-start(bf16[1,256,896]{2,1,0:T(8,128)(2,1)} %param.11) | copy-start | bytes 1376260
  126.4 29.3 %copy-start.9 = (f32[896]{0:T(1024)S(1)}, f32[896]{0:T(1024)}, u32[]{:S(2)}) copy-start(f32[896]{0:T(1024)} %param.13) | copy-start | bytes 10756
  (4 other events, 3.3 us)
Sparse Core Ops, SparseCore 0:
  107.0 41.5 reduce-scatter.1
where the time goes:
time: 166 us; the launch traced here: 165 us
  starting transfers between devices  70.4 us (42%)
  waiting for transfers between devices  38.9 us (23%)
  between operations  15.2 us (9%)
  matrix products  13.6 us (8%)
  local copies, waits for them, and re-layouts  11.7 us (7%)
  other arithmetic  9.12 us (5%)
  blocking collectives  5.76 us (3%)
    ppermute x14, starting transfers between devices, shifted(): return lax.ppermute(x, axis, pairs)  61.9 us
    reduce_scatter x1, waiting for transfers between devices, local(): lax.psum_scatter(partial_value, 'tp', scatter_dimension=2, tiled=True)  13 us
    ppermute x14, waiting for transfers between devices, shifted(): return lax.ppermute(x, axis, pairs)  12.3 us
    dot_general x1, matrix products, local(): jnp.dot(attended.reshape(seq_count * shard_len, query_width), out_weight,...  6.96 us
    all_to_all x1, waiting for transfers between devices, local(): lax.all_to_all(outgoing_keys, 'seq', split_axis=1, concat_axis=1, tiled=T...  6.96 us
    all_to_all x1, waiting for transfers between devices, local(): lax.all_to_all(outgoing_values, 'seq', split_axis=1, concat_axis=1, tiled...  6.61 us
    psum x1, blocking collectives, local(): squares = lax.psum(jnp.sum(branch * branch, axis=-1), 'tp')  5.76 us
    all_to_all x1, starting transfers between devices, local(): lax.all_to_all(outgoing_keys, 'seq', split_axis=1, concat_axis=1, tiled=T...  5.01 us
  transfers between devices with their start and end apart: 17, of which 10 were waited for; matrix products, arithmetic and copies ran while one was open for 12% of the time, Pallas kernels for 0%

commit v1 on v0

--- a/solution.py
+++ b/solution.py
@@ -1,11 +1,18 @@
+import functools
+
 import jax
 import jax.numpy as jnp
 from jax import lax
+from jax.experimental import pallas as pl
+from jax.experimental.pallas import tpu as pltpu
 from jax.sharding import PartitionSpec as P
 
 D = 3584
 HD = 256
 WINDOW = 4096
+MESH = pl.DeviceIdType.MESH
+LOG2E = 1.4426950408889634
+ROWS = 128
 
 
 soft_cap = 50.0
@@ -46,6 +53,15 @@
 
 def local(queries, key_rows, value_rows, residual, out_weight, post_scale, lengths, owners):
     seq_count, shard_len, query_width = queries.shape
+    seq_size = lax.axis_size("seq")
+    if (
+        seq_count == 1 and lax.axis_size("tp") == 4 and seq_size % 2 == 0
+        and seq_size * shard_len <= WINDOW
+    ):
+        return fused(
+            seq_size, queries, key_rows, value_rows, residual, out_weight, post_scale, lengths,
+            owners,
+        )
     kv_width = key_rows.shape[2]
     kv_local = kv_width // HD
     group_size = query_width // kv_width
@@ -128,6 +144,335 @@
     return (hidden_out, cache_keys, cache_values)
 
 
+def layer_kernel(
+    n, q_ref, k_ref, v_ref, res_ref, scale_ref, len_ref, own_ref, w_ref,
+    hid_ref, ck_ref, cv_ref,
+    kbuf, vbuf, wbuf, acc, den, att, to_sib, to_x, to_sib2, from_sib, from_x, from_sib2,
+    total, sq_out, sq_in,
+    send_sem, recv_sem, w_sem, rs_send, rs_recv, sq_send, sq_recv,
+):
+    nz = n // 2
+    me = lax.axis_index("seq")
+    t = lax.axis_index("tp")
+    z, y = me // 2, me % 2
+    x, c = t // 2, t % 2
+    sib = x * 2 + (1 - c)
+    across = (1 - x) * 2 + c
+    diagonal = (1 - x) * 2 + (1 - c)
+    shard = q_ref.shape[0]
+    heads = q_ref.shape[1] // HD
+    group = q_ref.shape[1] // k_ref.shape[1]
+    bufs = (kbuf, vbuf)
+    own = (k_ref, v_ref)
+
+    def w_copy(f):
+        return pltpu.make_async_copy(
+            w_ref.at[:, pl.ds(f * res_ref.shape[1], res_ref.shape[1])], wbuf.at[f], w_sem.at[f]
+        )
+
+    partner = z * 2 + (1 - y)
+    barrier = pltpu.get_barrier_semaphore()
+    for peer in (sib, across, diagonal):
+        pl.semaphore_signal(barrier, inc=1, device_id={"tp": peer}, device_id_type=MESH)
+    pl.semaphore_signal(barrier, inc=1, device_id={"seq": partner}, device_id_type=MESH)
+
+    @pl.when(z < nz - 1)
+    def _():
+        pl.semaphore_signal(barrier, inc=1, device_id={"seq": me + 2}, device_id_type=MESH)
+
+    @pl.when(z > 0)
+    def _():
+        pl.semaphore_signal(barrier, inc=1, device_id={"seq": me - 2}, device_id_type=MESH)
+
+    @pl.when((z > 0) & (z < nz - 1))
+    def _():
+        pl.semaphore_wait(barrier, 6)
+
+    @pl.when((z == 0) | (z == nz - 1))
+    def _():
+        pl.semaphore_wait(barrier, 5)
+
+    def routes(zo, yo, h, mine=False):
+        special = ((zo == 0) | (zo == nz - 1)) if h == 1 else False
+        line = (yo == y) | special
+        crossing = (yo == y) & ((zo == z) | jnp.logical_not(special))
+        origin = zo * 2 + yo
+        plan = (
+            (line & (zo <= z) & (z < nz - 1), me + 2),
+            (line & (zo >= z) & (z > 0), me - 2),
+            (crossing, partner),
+        )
+        out = []
+        for way, (go, to) in enumerate(plan):
+            copy = pltpu.make_async_remote_copy(
+                src_ref=own[h] if mine else bufs[h].at[origin],
+                dst_ref=bufs[h].at[origin],
+                send_sem=send_sem.at[origin, h, way],
+                recv_sem=recv_sem.at[origin, h],
+                device_id={"seq": to},
+                device_id_type=MESH,
+            )
+            out.append((go, copy))
+        return out
+
+    def start(zo, yo, h, mine=False):
+        for go, copy in routes(zo, yo, h, mine):
+            pl.when(go)(copy.start)
+
+    def handle(zo, yo, h):
+        routes(zo, yo, h)[0][1].wait_recv()
+        start(zo, yo, h)
+
+    start(z, y, 0, True)
+    start(z, y, 1, True)
+    for f in range(4):
+        w_copy(f).start()
+
+    def attend(keys, values, masked):
+        for h in range(heads):
+            cols = pl.ds((h // group) * HD, HD)
+            s = lax.dot_general(
+                q_ref[:, h * HD : (h + 1) * HD], keys[:, cols], (((1,), (1,)), ((), ())),
+                preferred_element_type=jnp.float32,
+            )
+            w = jnp.exp2(jnp.tanh(s * (HD ** (-0.5) / soft_cap)) * (soft_cap * LOG2E))
+            if masked:
+                keep = lax.broadcasted_iota(jnp.int32, w.shape, 0) >= lax.broadcasted_iota(
+                    jnp.int32, w.shape, 1
+                )
+                w = jnp.where(keep, w, 0.0)
+            folded = w[:, :128]
+            for i in range(1, w.shape[1] // 128):
+                folded = folded + w[:, i * 128 : (i + 1) * 128]
+            o = jnp.dot(w.astype(jnp.bfloat16), values[:, cols], preferred_element_type=jnp.float32)
+            if masked:
+                den[h] = folded
+                acc[h] = o
+            else:
+                den[h] += folded
+                acc[h] += o
+
+    attend(k_ref, v_ref, True)
+
+    def phase(d, carry):
+        e = d - 1
+        for h in (0, 1):
+            for sign in (-1, 1):
+                zz = z + sign * d
+                pl.when((zz >= 0) & (zz < nz))(functools.partial(handle, zz, y, h))
+        for h in (1, 0):
+            for sign in (-1, 1):
+                zz = z + sign * e
+                there = (zz >= 0) & (zz < nz)
+                if sign == 1:
+                    there = there & (e > 0)
+                pl.when(there)(functools.partial(handle, zz, 1 - y, h))
+
+        def one(i, carry):
+            zz = z - d + i
+            origin = zz * 2 + jnp.where(i == 0, y, 1 - y)
+
+            @pl.when((zz >= 0) & (origin < me))
+            def _():
+                attend(kbuf.at[origin], vbuf.at[origin], False)
+
+            return carry
+
+        lax.fori_loop(0, 2, one, 0)
+        return carry
+
+    lax.fori_loop(1, nz + 1, phase, 0)
+
+    for h in range(heads):
+        att[:, h * HD : (h + 1) * HD] = (
+            acc[h] / jnp.sum(den[h], axis=-1, keepdims=True)
+        ).astype(jnp.bfloat16)
+
+    chunks = shard // ROWS
+
+    def rs_copy(kind, r, src, dst, to):
+        return pltpu.make_async_remote_copy(
+            src_ref=src.at[r], dst_ref=dst.at[r], send_sem=rs_send.at[kind, r],
+            recv_sem=rs_recv.at[kind, r], device_id={"tp": to}, device_id_type=MESH,
+        )
+
+    def sib_copy(r):
+        return rs_copy(0, r, to_sib, from_sib, sib)
+
+    def x_copy(r):
+        return rs_copy(1, r, to_x, from_x, across)
+
+    def sib2_copy(r):
+        return rs_copy(2, r, to_sib2, from_sib2, sib)
+
+    def part(f, r):
+        rows = att[pl.ds(pl.multiple_of(r * ROWS, ROWS), ROWS), :]
+        return jnp.dot(rows, wbuf[f], preferred_element_type=jnp.float32)
+
+    for f in range(4):
+        w_copy(f).wait()
+
+    def first(r, carry):
+        to_sib[r] = part(diagonal, r).astype(jnp.bfloat16)
+        sib_copy(r).start()
+        return carry
+
+    def second(r, carry):
+        mine = part(across, r)
+        sib_copy(r).wait_recv()
+        to_x[r] = (mine + from_sib[r].astype(jnp.float32)).astype(jnp.bfloat16)
+        x_copy(r).start()
+        return carry
+
+    def third(r, carry):
+        to_sib2[r] = part(sib, r).astype(jnp.bfloat16)
+        sib2_copy(r).start()
+        return carry
+
+    def fourth(r, carry):
+        total[r] = part(t, r)
+        return carry
+
+    for step in (first, second, third, fourth):
+        lax.fori_loop(0, chunks, step, 0)
+
+    block_rows = shard // n
+    block = own_ref[0, 0] * 0
+    for b in range(n):
+        block = block + jnp.where(own_ref[0, b] == me, b, 0)
+    kbuf[me] = k_ref[...]
+    vbuf[me] = v_ref[...]
+    length = len_ref[0]
+    local_row = lax.broadcasted_iota(jnp.int32, (block_rows, k_ref.shape[1]), 0)
+    chosen = jnp.full(local_row.shape, block, jnp.int32)
+    bound = jnp.full(local_row.shape, length, jnp.int32)
+
+    def cache(origin, carry):
+        pos = local_row + chosen * block_rows + origin * shard
+        live = (pos < bound) & (pos >= bound - WINDOW)
+        spot = jnp.where(live, chosen, -1)
+        for buf, out in ((kbuf, ck_ref), (vbuf, cv_ref)):
+            got = jnp.zeros(local_row.shape, jnp.float32)
+            for b in range(n):
+                rows = buf[origin, b * block_rows : (b + 1) * block_rows, :]
+                got = jnp.where(spot == b, rows.astype(jnp.float32), got)
+            start_row = pl.multiple_of(origin * block_rows, block_rows)
+            out[pl.ds(start_row, block_rows), :] = got.astype(jnp.bfloat16)
+        return carry
+
+    lax.fori_loop(0, n, cache, 0)
+    rest = ck_ref.shape[0] - n * block_rows
+    if rest:
+        for out in (ck_ref, cv_ref):
+            out[n * block_rows :, :] = jnp.zeros((rest, k_ref.shape[1]), jnp.bfloat16)
+
+    for r in range(chunks):
+        sib2_copy(r).wait_recv()
+        x_copy(r).wait_recv()
+        branch = total[r] + from_sib2[r].astype(jnp.float32) + from_x[r].astype(jnp.float32)
+        total[r] = branch
+        squared = branch * branch
+        folded = squared[:, :128]
+        for i in range(1, squared.shape[1] // 128):
+            folded = folded + squared[:, i * 128 : (i + 1) * 128]
+        line = jnp.sum(folded.T, axis=0, keepdims=True)
+        sq_out[:, r * ROWS : (r + 1) * ROWS] = jnp.broadcast_to(line, (8, ROWS))
+
+    def sq_copy(i, to, slot):
+        return pltpu.make_async_remote_copy(
+            src_ref=sq_out, dst_ref=sq_in.at[slot], send_sem=sq_send.at[i],
+            recv_sem=sq_recv.at[slot], device_id={"tp": to}, device_id_type=MESH,
+        )
+
+    peers = (sib, across, diagonal)
+    for i, peer in enumerate(peers):
+        sq_copy(i, peer, t).start()
+    squares = sq_out[...]
+    for i, peer in enumerate(peers):
+        sq_copy(i, peer, peer).wait_recv()
+        squares = squares + sq_in[peer]
+    factor = lax.rsqrt(squares / D + norm_eps)
+    for r in range(chunks):
+        line = jnp.broadcast_to(factor[:1, r * ROWS : (r + 1) * ROWS], (128, ROWS))
+        spread = line.T
+        for i in range(res_ref.shape[1] // 128):
+            cols = slice(i * 128, (i + 1) * 128)
+            rows = slice(r * ROWS, (r + 1) * ROWS)
+            normed = total[r, :, cols] * spread * scale_ref[:, cols]
+            hid_ref[rows, cols] = (res_ref[rows, cols].astype(jnp.float32) + normed).astype(
+                jnp.bfloat16
+            )
+
+    for i, peer in enumerate(peers):
+        sq_copy(i, peer, t).wait_send()
+    for r in range(chunks):
+        sib_copy(r).wait_send()
+        x_copy(r).wait_send()
+        sib2_copy(r).wait_send()
+    for h in (0, 1):
+        for go, copy in routes(z, y, h, True):
+            pl.when(go)(copy.wait_send)
+
+    def drain(origin, carry):
+        @pl.when(origin != me)
+        def _():
+            for h in (0, 1):
+                for go, copy in routes(origin // 2, origin % 2, h):
+                    pl.when(go)(copy.wait_send)
+
+        return carry
+
+    lax.fori_loop(0, n, drain, 0)
+
+
+def fused(n, queries, key_rows, value_rows, residual, out_weight, post_scale, lengths, owners):
+    shard, q_width = queries.shape[1:]
+    kv_width = key_rows.shape[2]
+    width = residual.shape[2]
+    heads = q_width // HD
+    chunks = shard // ROWS
+    cache_rows = WINDOW // n
+    vmem = pl.BlockSpec(memory_space=pltpu.VMEM)
+    smem = pl.BlockSpec(memory_space=pltpu.SMEM)
+    half = pltpu.VMEM((chunks, ROWS, width), jnp.bfloat16)
+    hidden, ck, cv = pl.pallas_call(
+        functools.partial(layer_kernel, n),
+        out_shape=(
+            jax.ShapeDtypeStruct((shard, width), jnp.bfloat16),
+            jax.ShapeDtypeStruct((cache_rows, kv_width), jnp.bfloat16),
+            jax.ShapeDtypeStruct((cache_rows, kv_width), jnp.bfloat16),
+        ),
+        in_specs=[vmem] * 5 + [smem] * 2 + [pl.BlockSpec(memory_space=pl.ANY)],
+        out_specs=(vmem,) * 3,
+        scratch_shapes=[
+            pltpu.VMEM((n, shard, kv_width), jnp.bfloat16),
+            pltpu.VMEM((n, shard, kv_width), jnp.bfloat16),
+            pltpu.VMEM((4, q_width, width), jnp.bfloat16),
+            pltpu.VMEM((heads, shard, HD), jnp.float32),
+            pltpu.VMEM((heads, shard, 128), jnp.float32),
+            pltpu.VMEM((shard, q_width), jnp.bfloat16),
+            half, half, half, half, half, half,
+            pltpu.VMEM((chunks, ROWS, width), jnp.float32),
+            pltpu.VMEM((8, shard), jnp.float32),
+            pltpu.VMEM((4, 8, shard), jnp.float32),
+            pltpu.SemaphoreType.DMA((n, 2, 3)),
+            pltpu.SemaphoreType.DMA((n, 2)),
+            pltpu.SemaphoreType.DMA((4,)),
+            pltpu.SemaphoreType.DMA((3, chunks)),
+            pltpu.SemaphoreType.DMA((3, chunks)),
+            pltpu.SemaphoreType.DMA((3,)),
+            pltpu.SemaphoreType.DMA((4,)),
+        ],
+        compiler_params=pltpu.CompilerParams(
+            collective_id=0, has_side_effects=True, vmem_limit_bytes=48 * 1024 * 1024
+        ),
+    )(
+        queries[0], key_rows[0], value_rows[0], residual[0], post_scale[None], lengths, owners,
+        out_weight,
+    )
+    return hidden[None], ck[None], cv[None]
+
+
 def solution(mesh):
     placed = (
         P(None, "seq", "tp"),

time: 166 us -> 75.1 us (0.45)
  starting transfers between devices: 70.4 us -> 0 us
  Pallas kernels: 0 us -> 65.8 us
  waiting for transfers between devices: 38.9 us -> 0 us
  between operations: 15.2 us -> 1.29 us
  matrix products: 13.6 us -> 0 us
  other arithmetic: 9.12 us -> 0 us
  blocking collectives: 5.76 us -> 0 us
  local copies, waits for them, and re-layouts: 11.7 us -> 7.66 us
    pallas_call x0 -> x1, Pallas kernels: none -> 65.8 us  [fused(): pl.pallas_call(functools.partial(layer_kernel, n), out_shape=(jax.ShapeDt...]
    ppermute x14 -> x0, starting transfers between devices: 61.9 us -> none  [shifted(): return lax.ppermute(x, axis, pairs)]
    dot_general x13 -> x0, matrix products: 13.6 us -> none  [the longest x1 6.96 us: local(): jnp.dot(attended.reshape(seq_count * shard_len, query_width), out_weight,...]
    all_to_all x2 -> x0, waiting for transfers between devices: 13.6 us -> none  [the longest x1 6.96 us: local(): lax.all_to_all(outgoing_keys, 'seq', split_axis=1, concat_axis=1, tiled=T...]
    reduce_scatter x1 -> x0, waiting for transfers between devices: 13 us -> none  [local(): lax.psum_scatter(partial_value, 'tp', scatter_dimension=2, tiled=True)]
    ppermute x14 -> x0, waiting for transfers between devices: 12.3 us -> none  [shifted(): return lax.ppermute(x, axis, pairs)]
    all_to_all x2 -> x0, starting transfers between devices: 8.43 us -> none  [the longest x1 5.01 us: local(): lax.all_to_all(outgoing_keys, 'seq', split_axis=1, concat_axis=1, tiled=T...]
    psum x1 -> x0, blocking collectives: 5.76 us -> none  [local(): squares = lax.psum(jnp.sum(branch * branch, axis=-1), 'tp')]
  transfers between devices with their start and end apart: 17 -> 0, of which waited for: 10 -> 0; matrix products, arithmetic and copies ran while one was open for 12% -> 0% of each run, Pallas kernels for 0% -> 0%
where the time goes in v1:
time: 75.1 us; the launch traced here: 74.8 us
  Pallas kernels  65.8 us (88%)
  local copies, waits for them, and re-layouts  7.66 us (10%)
  between operations  1.29 us (2%)
    pallas_call x1, Pallas kernels, fused(): pl.pallas_call(functools.partial(layer_kernel, n), out_shape=(jax.ShapeDt...  65.8 us
    unnamed x13, local copies, waits for them, and re-layouts  6.97 us

profile of v1, /device:TPU:0, one launch (start us, length us, event | category | flops | bytes accessed | tf_op | source)
XLA Modules:
  0.0 74.8 jit_solution(4150948362929219865)
XLA Ops:
  1.3 0.7 broadcast_in_dim.12.scale_ref
  2.0 0.0 copy-start
  2.0 1.0 %copy-done = bf16[1,256,1024]{2,1,0:T(8,128)(2,1)S(1)} copy-done((bf16[1,256,1024]{2,1,0:T(8,128)(2,1)S(1)}, bf16[1,256,1024]{2,1,0:T(8,128)(2,1)}, u32[]{:S(2)}) %copy-start) | copy-done | bytes 524312
  3.0 0.0 copy-start.1
  3.0 1.0 %copy-done.1 = bf16[1,256,896]{2,1,0:T(8,128)(2,1)S(1)} copy-done((bf16[1,256,896]{2,1,0:T(8,128)(2,1)S(1)}, bf16[1,256,896]{2,1,0:T(8,128)(2,1)}, u32[]{:S(2)}) %copy-start.1) | copy-done | bytes 458776
  4.0 0.0 copy-start.2
  4.0 0.9 %copy-done.2 = bf16[1,256,512]{2,1,0:T(8,128)(2,1)S(1)} copy-done((bf16[1,256,512]{2,1,0:T(8,128)(2,1)S(1)}, bf16[1,256,512]{2,1,0:T(8,128)(2,1)}, u32[]{:S(2)}) %copy-start.2) | copy-done | bytes 262168
  5.0 0.0 copy-start.3
  5.0 0.9 %copy-done.3 = bf16[1,256,512]{2,1,0:T(8,128)(2,1)S(1)} copy-done((bf16[1,256,512]{2,1,0:T(8,128)(2,1)S(1)}, bf16[1,256,512]{2,1,0:T(8,128)(2,1)}, u32[]{:S(2)}) %copy-start.3) | copy-done | bytes 262168
  5.9 0.0 copy-start.4
  5.9 0.7 copy-done.4
  6.6 65.8 %shard_map.103 = (bf16[256,896]{1,0:T(8,128)(2,1)S(1)}, bf16[512,512]{1,0:T(8,128)(2,1)S(1)}, bf16[512,512]{1,0:T(8,128)(2,1)S(1)}) custom-call(bf16[256,1024]{1,0:T(8,128)(2,1)S(1)} %bitcast.7, bf16[256,512]{1,0:T(8,128)(2,1)S(1)} %bitcast.12, bf16[256,512]{1,0:T(8,128)(2,1)S(1)} %bitcast.13, bf16[256,896]{1,0:T(8,128)(2,1)S(1)} %bitcast.11, ...), custom_call_target="tpu_custom_call" | custom-call | tf_op jit(solution)/shard_map/pallas_call | solution.py:438
  72.4 0.8 %copy.15 = bf16[1,256,896]{2,1,0:T(8,128)(2,1)} copy(bf16[1,256,896]{2,1,0:T(8,128)(2,1)S(1)} %bitcast.10) | data formatting | bytes 917504
  73.2 0.8 %copy.16 = bf16[1,512,512]{2,1,0:T(8,128)(2,1)} copy(bf16[1,512,512]{2,1,0:T(8,128)(2,1)S(1)} %bitcast.9) | data formatting | bytes 1048576
  74.0 0.8 %copy.17 = bf16[1,512,512]{2,1,0:T(8,128)(2,1)} copy(bf16[1,512,512]{2,1,0:T(8,128)(2,1)S(1)} %bitcast.8) | data formatting | bytes 1048576
Async XLA Ops:
  2.0 1.0 %copy-start = (bf16[1,256,1024]{2,1,0:T(8,128)(2,1)S(1)}, bf16[1,256,1024]{2,1,0:T(8,128)(2,1)}, u32[]{:S(2)}) copy-start(bf16[1,256,1024]{2,1,0:T(8,128)(2,1)} %param.8) | copy-start | bytes 1572868
  3.0 1.0 %copy-start.1 = (bf16[1,256,896]{2,1,0:T(8,128)(2,1)S(1)}, bf16[1,256,896]{2,1,0:T(8,128)(2,1)}, u32[]{:S(2)}) copy-start(bf16[1,256,896]{2,1,0:T(8,128)(2,1)} %param.11) | copy-start | bytes 1376260
  4.0 0.9 %copy-start.2 = (bf16[1,256,512]{2,1,0:T(8,128)(2,1)S(1)}, bf16[1,256,512]{2,1,0:T(8,128)(2,1)}, u32[]{:S(2)}) copy-start(bf16[1,256,512]{2,1,0:T(8,128)(2,1)} %param.9) | copy-start | bytes 786436
  5.0 0.9 %copy-start.3 = (bf16[1,256,512]{2,1,0:T(8,128)(2,1)S(1)}, bf16[1,256,512]{2,1,0:T(8,128)(2,1)}, u32[]{:S(2)}) copy-start(bf16[1,256,512]{2,1,0:T(8,128)(2,1)} %param.10) | copy-start | bytes 786436
  5.9 0.7 copy-start.4

commit v2 on v1

--- a/solution.py
+++ b/solution.py
@@ -145,11 +145,12 @@
 
 
 def layer_kernel(
-    n, q_ref, k_ref, v_ref, res_ref, scale_ref, len_ref, own_ref, w_ref,
-    hid_ref, ck_ref, cv_ref,
+    n, q_hbm, k_hbm, v_hbm, res_hbm, scale_hbm, len_ref, own_hbm, w_ref,
+    hid_hbm, ck_hbm, cv_hbm,
+    hid_ref, ck_ref, cv_ref, q_ref, res_ref, scale_ref, own_ref, kstage, vstage, kgot, vgot,
     kbuf, vbuf, wbuf, acc, den, att, to_sib, to_x, to_sib2, from_sib, from_x, from_sib2,
     total, sq_out, sq_in,
-    send_sem, recv_sem, w_sem, rs_send, rs_recv, sq_send, sq_recv,
+    in_sem, send_sem, recv_sem, w_sem, rs_send, rs_recv, sq_send, sq_recv, cache_send, cache_recv, out_sem,
 ):
     nz = n // 2
     me = lax.axis_index("seq")
@@ -161,9 +162,21 @@
     diagonal = (1 - x) * 2 + (1 - c)
     shard = q_ref.shape[0]
     heads = q_ref.shape[1] // HD
-    group = q_ref.shape[1] // k_ref.shape[1]
+    kv_width = k_hbm.shape[1]
+    group = q_ref.shape[1] // kv_width
+    block_rows = shard // n
     bufs = (kbuf, vbuf)
-    own = (k_ref, v_ref)
+    loads = [
+        pltpu.make_async_copy(src, dst, in_sem.at[i])
+        for i, (src, dst) in enumerate(
+            (
+                (k_hbm, kbuf.at[me]), (v_hbm, vbuf.at[me]), (q_hbm, q_ref), (own_hbm, own_ref),
+                (res_hbm, res_ref), (scale_hbm, scale_ref),
+            )
+        )
+    ]
+    for load in loads:
+        load.start()
 
     def w_copy(f):
         return pltpu.make_async_copy(
@@ -174,38 +187,22 @@
     barrier = pltpu.get_barrier_semaphore()
     for peer in (sib, across, diagonal):
         pl.semaphore_signal(barrier, inc=1, device_id={"tp": peer}, device_id_type=MESH)
-    pl.semaphore_signal(barrier, inc=1, device_id={"seq": partner}, device_id_type=MESH)
-
-    @pl.when(z < nz - 1)
-    def _():
-        pl.semaphore_signal(barrier, inc=1, device_id={"seq": me + 2}, device_id_type=MESH)
-
-    @pl.when(z > 0)
-    def _():
-        pl.semaphore_signal(barrier, inc=1, device_id={"seq": me - 2}, device_id_type=MESH)
-
-    @pl.when((z > 0) & (z < nz - 1))
-    def _():
-        pl.semaphore_wait(barrier, 6)
-
-    @pl.when((z == 0) | (z == nz - 1))
-    def _():
-        pl.semaphore_wait(barrier, 5)
-
-    def routes(zo, yo, h, mine=False):
-        special = ((zo == 0) | (zo == nz - 1)) if h == 1 else False
+    for hop in range(1, n):
+        pl.semaphore_signal(
+            barrier, inc=1, device_id={"seq": lax.rem(me + hop, n)}, device_id_type=MESH
+        )
+    pl.semaphore_wait(barrier, n + 2)
+
+    def routes(zo, yo, h):
+        special = ((zo == 0) & (yo == 0)) if h == 1 else False
         line = (yo == y) | special
-        crossing = (yo == y) & ((zo == z) | jnp.logical_not(special))
+        crossing = (yo == y) & (zo + y <= z) & ((zo == z) | jnp.logical_not(special))
         origin = zo * 2 + yo
-        plan = (
-            (line & (zo <= z) & (z < nz - 1), me + 2),
-            (line & (zo >= z) & (z > 0), me - 2),
-            (crossing, partner),
-        )
+        plan = ((line & (zo <= z) & (z < nz - 1), me + 2), (crossing, partner))
         out = []
         for way, (go, to) in enumerate(plan):
             copy = pltpu.make_async_remote_copy(
-                src_ref=own[h] if mine else bufs[h].at[origin],
+                src_ref=bufs[h].at[origin],
                 dst_ref=bufs[h].at[origin],
                 send_sem=send_sem.at[origin, h, way],
                 recv_sem=recv_sem.at[origin, h],
@@ -215,18 +212,21 @@
             out.append((go, copy))
         return out
 
-    def start(zo, yo, h, mine=False):
-        for go, copy in routes(zo, yo, h, mine):
+    def start(zo, yo, h):
+        for go, copy in routes(zo, yo, h):
             pl.when(go)(copy.start)
 
     def handle(zo, yo, h):
         routes(zo, yo, h)[0][1].wait_recv()
         start(zo, yo, h)
 
-    start(z, y, 0, True)
-    start(z, y, 1, True)
+    for h in (0, 1):
+        loads[h].wait()
+        start(z, y, h)
     for f in range(4):
         w_copy(f).start()
+    loads[2].wait()
+    loads[3].wait()
 
     def attend(keys, values, masked):
         for h in range(heads):
@@ -252,21 +252,51 @@
                 den[h] += folded
                 acc[h] += o
 
-    attend(k_ref, v_ref, True)
+    stages = ((kbuf, kstage, kgot), (vbuf, vstage, vgot))
+
+    def cache_copy(h, to, slot):
+        return pltpu.make_async_remote_copy(
+            src_ref=stages[h][1].at[to], dst_ref=stages[h][2].at[slot],
+            send_sem=cache_send.at[to, h], recv_sem=cache_recv.at[slot, h],
+            device_id={"seq": to}, device_id_type=MESH,
+        )
+
+    def select(buf, origin, chosen):
+        got = jnp.zeros(chosen.shape, jnp.float32)
+        for b in range(n):
+            rows = buf[origin, b * block_rows : (b + 1) * block_rows, :]
+            got = jnp.where(chosen == b, rows.astype(jnp.float32), got)
+        return got.astype(jnp.bfloat16)
+
+    def owned(device):
+        block = own_ref[0, 0] * 0
+        for b in range(n):
+            block = block + jnp.where(own_ref[0, b] == device, b, 0)
+        return jnp.full((block_rows, kv_width), block, jnp.int32)
+
+    def stage(to, carry):
+        chosen = owned(to)
+        for buf, staged, _ in stages:
+            staged[to] = select(buf, me, chosen)
+        return carry
+
+    lax.fori_loop(0, me, stage, 0)
+    attend(kbuf.at[me], vbuf.at[me], True)
+
+    def post(to, carry):
+        for h in (0, 1):
+            cache_copy(h, to, me).start()
+        return carry
+
+    lax.fori_loop(0, me, post, 0)
 
     def phase(d, carry):
         e = d - 1
         for h in (0, 1):
-            for sign in (-1, 1):
-                zz = z + sign * d
-                pl.when((zz >= 0) & (zz < nz))(functools.partial(handle, zz, y, h))
+            pl.when(z - d >= 0)(functools.partial(handle, z - d, y, h))
         for h in (1, 0):
-            for sign in (-1, 1):
-                zz = z + sign * e
-                there = (zz >= 0) & (zz < nz)
-                if sign == 1:
-                    there = there & (e > 0)
-                pl.when(there)(functools.partial(handle, zz, 1 - y, h))
+            there = (z - e >= 0) & ((e > 0) | (y == 1))
+            pl.when(there)(functools.partial(handle, z - e, 1 - y, h))
 
         def one(i, carry):
             zz = z - d + i
@@ -336,35 +366,43 @@
     for step in (first, second, third, fourth):
         lax.fori_loop(0, chunks, step, 0)
 
-    block_rows = shard // n
-    block = own_ref[0, 0] * 0
-    for b in range(n):
-        block = block + jnp.where(own_ref[0, b] == me, b, 0)
-    kbuf[me] = k_ref[...]
-    vbuf[me] = v_ref[...]
-    length = len_ref[0]
-    local_row = lax.broadcasted_iota(jnp.int32, (block_rows, k_ref.shape[1]), 0)
-    chosen = jnp.full(local_row.shape, block, jnp.int32)
-    bound = jnp.full(local_row.shape, length, jnp.int32)
+    chosen = owned(me)
+    local_row = lax.broadcasted_iota(jnp.int32, chosen.shape, 0)
+    bound = jnp.full(chosen.shape, len_ref[0], jnp.int32)
 
     def cache(origin, carry):
         pos = local_row + chosen * block_rows + origin * shard
         live = (pos < bound) & (pos >= bound - WINDOW)
-        spot = jnp.where(live, chosen, -1)
-        for buf, out in ((kbuf, ck_ref), (vbuf, cv_ref)):
-            got = jnp.zeros(local_row.shape, jnp.float32)
-            for b in range(n):
-                rows = buf[origin, b * block_rows : (b + 1) * block_rows, :]
-                got = jnp.where(spot == b, rows.astype(jnp.float32), got)
-            start_row = pl.multiple_of(origin * block_rows, block_rows)
-            out[pl.ds(start_row, block_rows), :] = got.astype(jnp.bfloat16)
+        start_row = pl.multiple_of(origin * block_rows, block_rows)
+
+        @pl.when(origin <= me)
+        def _():
+            spot = jnp.where(live, chosen, -1)
+            for (buf, _, _), out in zip(stages, (ck_ref, cv_ref)):
+                out[pl.ds(start_row, block_rows), :] = select(buf, origin, spot)
+
+        @pl.when(origin > me)
+        def _():
+            for h, out in enumerate((ck_ref, cv_ref)):
+                cache_copy(h, origin, origin).wait_recv()
+                got = stages[h][2][origin].astype(jnp.float32)
+                out[pl.ds(start_row, block_rows), :] = jnp.where(live, got, 0.0).astype(
+                    jnp.bfloat16
+                )
+
         return carry
 
     lax.fori_loop(0, n, cache, 0)
     rest = ck_ref.shape[0] - n * block_rows
     if rest:
         for out in (ck_ref, cv_ref):
-            out[n * block_rows :, :] = jnp.zeros((rest, k_ref.shape[1]), jnp.bfloat16)
+            out[n * block_rows :, :] = jnp.zeros((rest, kv_width), jnp.bfloat16)
+    outs = [
+        pltpu.make_async_copy(src, dst, out_sem.at[i])
+        for i, (src, dst) in enumerate(((ck_ref, ck_hbm), (cv_ref, cv_hbm), (hid_ref, hid_hbm)))
+    ]
+    outs[0].start()
+    outs[1].start()
 
     for r in range(chunks):
         sib2_copy(r).wait_recv()
@@ -391,6 +429,8 @@
     for i, peer in enumerate(peers):
         sq_copy(i, peer, peer).wait_recv()
         squares = squares + sq_in[peer]
+    loads[4].wait()
+    loads[5].wait()
     factor = lax.rsqrt(squares / D + norm_eps)
     for r in range(chunks):
         line = jnp.broadcast_to(factor[:1, r * ROWS : (r + 1) * ROWS], (128, ROWS))
@@ -398,31 +438,54 @@
         for i in range(res_ref.shape[1] // 128):
             cols = slice(i * 128, (i + 1) * 128)
             rows = slice(r * ROWS, (r + 1) * ROWS)
-            normed = total[r, :, cols] * spread * scale_ref[:, cols]
+            normed = total[r, :, cols] * spread * scale_ref[cols].reshape(1, 128)
             hid_ref[rows, cols] = (res_ref[rows, cols].astype(jnp.float32) + normed).astype(
                 jnp.bfloat16
             )
 
+    outs[2].start()
     for i, peer in enumerate(peers):
         sq_copy(i, peer, t).wait_send()
     for r in range(chunks):
         sib_copy(r).wait_send()
         x_copy(r).wait_send()
         sib2_copy(r).wait_send()
-    for h in (0, 1):
-        for go, copy in routes(z, y, h, True):
-            pl.when(go)(copy.wait_send)
 
     def drain(origin, carry):
-        @pl.when(origin != me)
-        def _():
-            for h in (0, 1):
-                for go, copy in routes(origin // 2, origin % 2, h):
-                    pl.when(go)(copy.wait_send)
-
-        return carry
-
-    lax.fori_loop(0, n, drain, 0)
+        for h in (0, 1):
+            for go, copy in routes(origin // 2, origin % 2, h):
+                pl.when(go)(copy.wait_send)
+        return carry
+
+    lax.fori_loop(0, me + 1, drain, 0)
+
+    def settle(to, carry):
+        for h in (0, 1):
+            cache_copy(h, to, me).wait_send()
+        return carry
+
+    lax.fori_loop(0, me, settle, 0)
+    for out in outs:
+        out.wait()
+
+
+def put_out(*refs):
+    count = (len(refs) - 1) // 3
+    sems = refs[-1]
+    copies = [
+        (
+            pltpu.make_async_copy(refs[i], refs[2 * count + i], sems.at[0, i]),
+            pltpu.make_async_copy(refs[2 * count + i], refs[count + i], sems.at[1, i]),
+        )
+        for i in range(count)
+    ]
+    for read, _ in copies:
+        read.start()
+    for read, write in copies:
+        read.wait()
+        write.start()
+    for _, write in copies:
+        write.wait()
 
 
 def fused(n, queries, key_rows, value_rows, residual, out_weight, post_scale, lengths, owners):
@@ -432,8 +495,9 @@
     heads = q_width // HD
     chunks = shard // ROWS
     cache_rows = WINDOW // n
-    vmem = pl.BlockSpec(memory_space=pltpu.VMEM)
     smem = pl.BlockSpec(memory_space=pltpu.SMEM)
+    apart = pl.BlockSpec(memory_space=pl.ANY)
+    owned_rows = pltpu.VMEM((n, shard // n, kv_width), jnp.bfloat16)
     half = pltpu.VMEM((chunks, ROWS, width), jnp.bfloat16)
     hidden, ck, cv = pl.pallas_call(
         functools.partial(layer_kernel, n),
@@ -442,9 +506,17 @@
             jax.ShapeDtypeStruct((cache_rows, kv_width), jnp.bfloat16),
             jax.ShapeDtypeStruct((cache_rows, kv_width), jnp.bfloat16),
         ),
-        in_specs=[vmem] * 5 + [smem] * 2 + [pl.BlockSpec(memory_space=pl.ANY)],
-        out_specs=(vmem,) * 3,
+        in_specs=[apart] * 5 + [smem] + [apart] * 2,
+        out_specs=(apart,) * 3,
         scratch_shapes=[
+            pltpu.VMEM((shard, width), jnp.bfloat16),
+            pltpu.VMEM((cache_rows, kv_width), jnp.bfloat16),
+            pltpu.VMEM((cache_rows, kv_width), jnp.bfloat16),
+            pltpu.VMEM((shard, q_width), jnp.bfloat16),
+            pltpu.VMEM((shard, width), jnp.bfloat16),
+            pltpu.VMEM((width,), jnp.float32),
+            pltpu.SMEM((1, n), jnp.int32),
+            owned_rows, owned_rows, owned_rows, owned_rows,
             pltpu.VMEM((n, shard, kv_width), jnp.bfloat16),
             pltpu.VMEM((n, shard, kv_width), jnp.bfloat16),
             pltpu.VMEM((4, q_width, width), jnp.bfloat16),
@@ -455,21 +527,34 @@
             pltpu.VMEM((chunks, ROWS, width), jnp.float32),
             pltpu.VMEM((8, shard), jnp.float32),
             pltpu.VMEM((4, 8, shard), jnp.float32),
-            pltpu.SemaphoreType.DMA((n, 2, 3)),
+            pltpu.SemaphoreType.DMA((6,)),
+            pltpu.SemaphoreType.DMA((n, 2, 2)),
             pltpu.SemaphoreType.DMA((n, 2)),
             pltpu.SemaphoreType.DMA((4,)),
             pltpu.SemaphoreType.DMA((3, chunks)),
             pltpu.SemaphoreType.DMA((3, chunks)),
             pltpu.SemaphoreType.DMA((3,)),
             pltpu.SemaphoreType.DMA((4,)),
+            pltpu.SemaphoreType.DMA((n, 2)),
+            pltpu.SemaphoreType.DMA((n, 2)),
+            pltpu.SemaphoreType.DMA((3,)),
         ],
         compiler_params=pltpu.CompilerParams(
-            collective_id=0, has_side_effects=True, vmem_limit_bytes=48 * 1024 * 1024
+            collective_id=0, has_side_effects=True, vmem_limit_bytes=60 * 1024 * 1024
         ),
     )(
-        queries[0], key_rows[0], value_rows[0], residual[0], post_scale[None], lengths, owners,
+        queries[0], key_rows[0], value_rows[0], residual[0], post_scale, lengths, owners,
         out_weight,
     )
+    made = (hidden, ck, cv)
+    hidden, ck, cv = pl.pallas_call(
+        put_out,
+        out_shape=tuple(jax.ShapeDtypeStruct(a.shape, a.dtype) for a in made),
+        in_specs=[apart] * len(made),
+        out_specs=(apart,) * len(made),
+        scratch_shapes=[pltpu.VMEM(a.shape, a.dtype) for a in made]
+        + [pltpu.SemaphoreType.DMA((2, len(made)))],
+    )(*made)
     return hidden[None], ck[None], cv[None]
 
 

time: 75.1 us -> 67.4 us (0.90)
  the two profiles are of different devices: /device:TPU:0 before, /device:TPU:25 now
where the time goes in v2:
time: 67.4 us; the launch traced here: 67.3 us
  Pallas kernels  66 us (98%)
  between operations  1.29 us (2%)
    pallas_call x1, Pallas kernels, fused(): pl.pallas_call(functools.partial(layer_kernel, n), out_shape=(jax.ShapeDt...  63.8 us
    pallas_call x1, Pallas kernels, fused(): pl.pallas_call(put_out, out_shape=tuple((jax.ShapeDtypeStruct(a.shape, a....  2.2 us

profile of v2, /device:TPU:25, one launch (start us, length us, event | category | flops | bytes accessed | tf_op | source)
XLA Modules:
  0.0 67.3 jit_solution(12502396550537452660)
XLA Ops:
  1.3 63.8 %shard_map.103 = (bf16[256,896]{1,0:T(8,128)(2,1)}, bf16[512,512]{1,0:T(8,128)(2,1)}, bf16[512,512]{1,0:T(8,128)(2,1)}) custom-call(bf16[256,1024]{1,0:T(8,128)(2,1)} %bitcast.7, bf16[256,512]{1,0:T(8,128)(2,1)} %bitcast.9, bf16[256,512]{1,0:T(8,128)(2,1)} %bitcast.10, bf16[256,896]{1,0:T(8,128)(2,1)} %bitcast.8, f32[896]{0:T(1024)} %scale_hbm.1, ...), custom_call_target="tpu_custom_call" | custom-call | tf_op jit(solution)/shard_map/pallas_call | solution.py:502
  65.1 2.2 %shard_map.104 = (bf16[256,896]{1,0:T(8,128)(2,1)}, bf16[512,512]{1,0:T(8,128)(2,1)}, bf16[512,512]{1,0:T(8,128)(2,1)}) custom-call(bf16[256,896]{1,0:T(8,128)(2,1)} %get-tuple-element.9.refs_0_, bf16[512,512]{1,0:T(8,128)(2,1)} %get-tuple-element.10.refs_1_, bf16[512,512]{1,0:T(8,128)(2,1)} %get-tuple-element.11.refs_2_), custom_call_target="tpu_custom_call" | custom-call | tf_op jit(solution)/shard_map/pallas_call | solution.py:550
